TPU v7x, 32 devices: a whole 2x2x4 slice. The times are simulated.
32 devices in a mesh: cp: 32 (over z, y, x, core).
Axes of the slice: x: 2, y: 2, z: 4, core: 2. Of those that a mesh axis runs over, the one named last changes fastest.
Arguments:
- raw_inputs: bfloat16 [3584, 57344], P(None, 'cp'), may hold values from -6 to 6
- state_maps: bfloat16 [128, 57344], P(None, 'cp'), may hold values from -6 to 6
- step_size: float32 [56, 57344], P(None, 'cp'), may hold values from 0 to 1, as said below
- log_decay: float32 [56, 57344], P(None, 'cp'), may hold values from -2 to 0, as said below
- conv_weight: float32 [4, 3584], replicated, may hold values from -3 to 3
- conv_bias: float32 [3584], replicated, may hold values from -3 to 3
- skip_gain: float32 [56], replicated, may hold values from 0.5 to 1.5
Outputs:
- layer_output: bfloat16 [3584, 57344], P(None, 'cp')
Inputs may be any that keep to these rules, and one draw needn't show every extreme that they name: step_size is positive. log_decay is never positive.
All inputs are finite; a program needn't handle non-finite values.
Results may differ from a plain program's by a relative error of at most 0.0058.
Values may be sent and summed in bfloat16 or wider, within the bound.
A program may use at most 192 MiB of HBM per device.

v0:
```python
import jax
import jax.numpy as jnp
from jax import lax
from jax.sharding import PartitionSpec as P

BLOCK = 256


def shifted(value, axis, steps):
    count = lax.axis_size(axis)
    initial, last = (max(0, -steps), min(count, count - steps))
    return lax.ppermute(value, axis, [(source, source + steps) for source in range(initial, last)])


def block_local(block_inputs, block_maps, block_sums, block_steps, state_dim, skip_gain):
    key_rows = block_maps[:state_dim]
    query_rows = block_maps[state_dim:]
    affinity = jnp.einsum("ni,nj->ij", query_rows, key_rows, preferred_element_type=jnp.float32)
    length = block_sums.shape[1]
    causal = lax.broadcasted_iota(jnp.int32, (length, length), 0) >= lax.broadcasted_iota(
        jnp.int32, (length, length), 1
    )
    decay_gaps = jnp.where(causal[None], block_sums[:, :, None] - block_sums[:, None, :], 0.0)
    weights = jnp.where(
        causal[None], affinity[None] * jnp.exp(decay_gaps) * block_steps[:, None, :], 0.0
    ).astype(jnp.bfloat16)
    local_out = jnp.einsum(
        "hij,hpj->hpi", weights, block_inputs, preferred_element_type=jnp.float32
    )
    return local_out + skip_gain[:, None, None] * block_inputs.astype(jnp.float32)


def block_carried(block_maps, block_sums, block_entering, state_dim):
    query_rows = block_maps[state_dim:]
    carried = jnp.einsum(
        "hnp,ni->hpi", block_entering, query_rows, preferred_element_type=jnp.float32
    )
    return carried * jnp.exp(block_sums)[:, None, :]


def merge_rows(earlier_part, later_part):
    return (earlier_part[0] * later_part[0], later_part[0] * earlier_part[1] + later_part[1])


def local(raw_inputs, state_maps, step_size, log_decay, conv_weight, conv_bias, skip_gain):
    conv_taps = conv_weight.shape[0]
    channels = raw_inputs.shape[0]
    row_count = raw_inputs.shape[1]
    head_count = skip_gain.shape[0]
    head_dim = channels // head_count
    state_dim = state_maps.shape[0] // 2
    block_count = row_count // BLOCK
    prior_rows = shifted(raw_inputs[:, row_count - (conv_taps - 1) :], "cp", 1)
    extended = jnp.concatenate([prior_rows, raw_inputs], axis=1)
    convolved = jnp.broadcast_to(conv_bias[:, None], (channels, row_count))
    for offset in range(conv_taps):
        convolved = convolved + conv_weight[offset][:, None] * extended[
            :, offset : offset + row_count
        ].astype(jnp.float32)
    values = jax.nn.silu(convolved).astype(jnp.bfloat16)
    inputs = values.reshape(head_count, head_dim, row_count)
    sums = jnp.cumsum(log_decay.reshape(head_count, block_count, BLOCK), axis=2)
    steps = step_size.reshape(head_count, block_count, BLOCK)

    def block_pieces(block_index):
        lower = block_index * BLOCK
        return (
            inputs[:, :, lower : lower + BLOCK],
            state_maps[:, lower : lower + BLOCK],
            sums[:, block_index],
            steps[:, block_index],
        )

    running = jnp.zeros((head_count, state_dim, head_dim), jnp.float32)
    device_decay = jnp.ones((head_count,), jnp.float32)
    entering_list = []
    before_list = []
    for block_index in range(block_count):
        piece_in, piece_map, piece_sum, piece_step = block_pieces(block_index)
        block_end = piece_sum[:, BLOCK - 1 :]
        scaled = (
            piece_map[None, :state_dim].astype(jnp.float32)
            * (jnp.exp(block_end - piece_sum) * piece_step)[:, None, :]
        ).astype(jnp.bfloat16)
        block_state = jnp.einsum(
            "hnj,hpj->hnp", scaled, piece_in, preferred_element_type=jnp.float32
        )
        block_decay = jnp.exp(block_end[:, 0])
        entering_list.append(running)
        before_list.append(device_decay)
        running = block_decay[:, None, None] * running + block_state
        device_decay = device_decay * block_decay
    peers = lax.axis_size("cp")
    rows_each = head_count * state_dim // peers
    send_state = running.reshape(peers, rows_each * head_dim)
    send_decay = jnp.repeat(device_decay, state_dim).reshape(peers, rows_each)
    got_state, got_decay = (
        lax.all_to_all(send_state, "cp", split_axis=0, concat_axis=0, tiled=True),
        lax.all_to_all(send_decay, "cp", split_axis=0, concat_axis=0, tiled=True),
    )
    wide_decay = jnp.repeat(got_decay, head_dim, axis=1)
    scan_decay, scan_state = lax.associative_scan(merge_rows, (wide_decay, got_state), axis=0)
    before_state = jnp.concatenate([jnp.zeros_like(scan_state[:1]), scan_state[:-1]], axis=0)
    returned = lax.all_to_all(before_state, "cp", split_axis=0, concat_axis=0, tiled=True)
    incoming = returned.reshape(head_count, state_dim, head_dim)
    result_list = []
    for block_index in range(block_count):
        piece_in, piece_map, piece_sum, piece_step = block_pieces(block_index)
        entering_b = (
            entering_list[block_index] + before_list[block_index][:, None, None] * incoming
        ).astype(jnp.bfloat16)
        local_part = block_local(piece_in, piece_map, piece_sum, piece_step, state_dim, skip_gain)
        result_list.append(
            (local_part + block_carried(piece_map, piece_sum, entering_b, state_dim)).astype(
                jnp.bfloat16
            )
        )
    return jnp.concatenate(result_list, axis=2).reshape(channels, row_count)


def solution(mesh):
    placed = (P(None, "cp"), P(None, "cp"), P(None, "cp"), P(None, "cp"), P(), P(), P())
    return jax.shard_map(
        local, mesh=mesh, in_specs=placed, out_specs=P(None, "cp"), check_vma=False
    )
```

profile of v0, /device:TPU:29, one launch (start us, length us, event | category | flops | bytes accessed | tf_op | source)
XLA Modules:
  0.0 202.3 jit_solution(10952224345122486446)
XLA Ops:
  0.0 1.5 slice.337
  1.9 3.7 %collective-permute-start = (bf16[3584,3]{0,1:T(4,128)(2,1)S(1)}, bf16[3584,3]{0,1:T(4,128)(2,1)S(1)}, u32[]{:S(2)}, u32[]{:S(2)}) collective-permute-start(bf16[3584,3]{0,1:T(4,128)(2,1)S(1)} %copy.125), channel_id=1, source_target_pairs={{0,1},{1,2},{2,3},{3,4},{4,5},{5,6},{6,7},{7,8},{8,9},{9,10},{10,1... | collective-permute-start | bytes 64520 | tf_op jit(solution)/shard_map/ppermute | solution.py:12
  5.6 1.2 reshape.222
  6.8 4.2 %reduce-window.6 = f32[56,7,2,128]{3,0,1,2:T(8,128)S(1)} reduce-window(f32[56,7,2,128]{3,0,1,2:T(8,128)S(1)} %copy.96, f32[]{:T(128)} %constant.5.clone.1), window={size=1x1x1x128 pad=0_0x0_0x0_0x127_0}, to_apply=%region_0.1 | reduce-window | flops 12744704 | bytes 802820 | tf_op jit(solution)/shard_map/reduce-window
  12.3 0.8 exponential_bitcast_fusion.3
  14.0 0.5 fusion.173
  14.6 0.7 all_to_all.24
  15.3 4.6 %all-to-all-start.1 = ((f32[32,1,112]{2,1,0:T(1,128)}), f32[32,1,112]{2,1,0:T(1,128)S(1)}, u32[]{:S(2)}, u32[]{:S(2)}) async-start(f32[32,1,112]{2,1,0:T(1,128)} %all_to_all.24), calls=%async_computation.1 | async-start | bytes 32768 | tf_op jit(solution)/shard_map/all_to_all | solution.py:99
  20.0 0.9 exponential_bitcast_fusion
  21.1 0.5 copy.95
  21.5 41.3 %multiply_convert_fusion = bf16[3584,1792]{1,0:T(8,128)(2,1)} fusion(bf16[3584,1792]{1,0:T(8,128)(2,1)} %param.7, bf16[3584,3]{1,0:T(8,128)(2,1)S(1)} %copy.95, f32[3584]{0:T(1024)S(1)} %get-tuple-element.7, f32[3584]{0:T(1024)S(1)} %get-tuple-element.8, f32[3584]{0:T(1024)S(1)} %get-tuple-element.6, f32[3584]{0:T(1024)S(1)} %get-tuple-element.5, ...), kind=kLoop, calls=%fused_computation | loop fusion | flops 166985728 | bytes 25783296 | tf_op jit(solution)/shard_map/convert_element_type | solution.py:60
  62.9 2.3 %fusion.51 = f32[56,64,64]{2,1,0:T(8,128)S(1)} fusion(f32[56,256]{1,0:T(8,128)S(1)} %get-tuple-element.32, f32[64,256]{1,0:T(8,128)S(1)} %get-tuple-element.18, bf16[56,64,1792]{2,1,0:T(8,128)(2,1)} %bitcast.93), kind=kOutput, calls=%fused_computation.76 | convolution fusion | flops 119275520 | bytes 2875392 | tf_op jit(solution)/shard_map/hnj,hpj->hnp/dot_general | solution.py:85
  65.2 3.3 %multiply_add_fusion.5 = f32[56,64,64]{2,1,0:T(8,128)S(1)} fusion(f32[56,64,64]{2,1,0:T(8,128)S(1)} %fusion.51, bf16[56,64,1792]{2,1,0:T(8,128)(2,1)} %bitcast.94, f32[56,256]{1,0:T(8,128)S(1)} %get-tuple-element.43, f32[64,256]{1,0:T(8,128)S(1)} %get-tuple-element.23, f32[56]{0:T(128)S(1)} %get-tuple-element.68, f32[56]{0:T(128)S(1)} %get-tuple-element.75), kind=kOutput, calls=%fused_computation.106 | convolution fusion | flops 119963648 | bytes 3793344 | tf_op jit(solution)/shard_map/hnj,hpj->hnp/dot_general | solution.py:85
  68.5 2.8 %multiply_add_fusion.4 = f32[56,64,64]{2,1,0:T(8,128)S(1)} fusion(f32[56,64,64]{2,1,0:T(8,128)S(1)} %multiply_add_fusion.5, bf16[56,64,1792]{2,1,0:T(8,128)(2,1)} %bitcast.95, f32[56,256]{1,0:T(8,128)S(1)} %get-tuple-element.41, f32[64,256]{1,0:T(8,128)S(1)} %get-tuple-element.22, f32[56]{0:T(128)S(1)} %get-tuple-element.76), kind=kOutput, calls=%fused_computation.103 | convolution fusion | flops 119734272 | bytes 3793120 | tf_op jit(solution)/shard_map/hnj,hpj->hnp/dot_general | solution.py:85
  71.4 0.6 multiply_add_fusion.3
  72.1 0.6 multiply_add_fusion.2
  72.7 0.6 multiply_add_fusion.1
  73.4 0.5 copy-done.5
  74.0 0.7 copy-done.7
  74.7 0.6 multiply_add_fusion
  75.3 2.1 %all_to_all.30 = f32[32,1,7168]{2,1,0:T(1,128)} reshape(f32[56,64,64]{2,1,0:T(8,128)S(1)} %multiply_add_fusion) | data formatting | bytes 1835008 | tf_op jit(solution)/shard_map/all_to_all | solution.py:98
  77.4 5.9 %all-to-all-start = ((f32[32,1,7168]{2,1,0:T(1,128)}), f32[32,1,7168]{2,1,0:T(1,128)}, u32[]{:S(2)}, u32[]{:S(2)}) async-start(f32[32,1,7168]{2,1,0:T(1,128)} %all_to_all.30), calls=%async_computation | async-start | bytes 1835008 | tf_op jit(solution)/shard_map/all_to_all | solution.py:98
  83.3 0.5 broadcast_in_dim.173
  83.9 0.5 reshape.225
  84.8 1.4 slice.389
  86.2 1.4 slice.385
  87.7 16.9 %all-to-all-done = f32[32,1,7168]{2,1,0:T(1,128)} async-done(((f32[32,1,7168]{2,1,0:T(1,128)}), f32[32,1,7168]{2,1,0:T(1,128)}, u32[]{:S(2)}, u32[]{:S(2)}) %all-to-all-start) | async-done | bytes 917536 | tf_op jit(solution)/shard_map/all_to_all | solution.py:98
  104.6 1.3 copy.149
  106.3 1.4 slice.387
  107.8 1.5 slice.386
  109.2 1.3 fusion.168
  110.9 0.8 slice.392
  111.7 1.0 fusion.170
  115.9 0.8 slice_bitcast_fusion.7
  117.1 1.9 copy.108
  119.0 5.8 %all-to-all-start.2 = ((f32[32,1,7168]{2,1,0:T(1,128)}), f32[32,1,7168]{2,1,0:T(1,128)S(1)}, u32[]{:S(2)}, u32[]{:S(2)}) async-start(f32[32,1,7168]{2,1,0:T(1,128)} %copy.108), calls=%async_computation.2 | async-start | bytes 1835008 | tf_op jit(solution)/shard_map/all_to_all | solution.py:104
  124.9 0.6 iota_compare_fusion
  125.5 0.9 fusion.154
  126.4 0.9 fusion.146
  127.3 0.9 fusion.143
  128.2 0.9 fusion.140
  129.1 0.9 fusion.137
  130.1 0.9 fusion.134
  131.2 14.8 %all-to-all-done.2 = f32[32,1,7168]{2,1,0:T(1,128)S(1)} async-done(((f32[32,1,7168]{2,1,0:T(1,128)}), f32[32,1,7168]{2,1,0:T(1,128)S(1)}, u32[]{:S(2)}, u32[]{:S(2)}) %all-to-all-start.2) | async-done | bytes 917536 | tf_op jit(solution)/shard_map/all_to_all | solution.py:104
  146.0 2.2 %reduce.11 = f32[32,7168]{1,0:T(8,128)S(1)} reduce(f32[32,1,7168]{2,1,0:T(1,128)S(1)} %all-to-all-done.2, f32[]{:T(128)} %constant.32), dimensions={1}, to_apply=%all_to_all.29.reduce_sub_computation | reduce | bytes 1835012 | tf_op jit(solution)/shard_map/all_to_all | solution.py:104
  148.2 0.5 reshape.226
  148.7 0.7 fusion.117
  149.4 0.8 copy-done.15
  150.2 1.4 fusion.105
  151.7 1.3 fusion.106
  153.2 1.3 fusion.107
  154.5 0.5 copy-done.4
  155.0 1.3 fusion.108
  156.3 0.5 copy-done.6
  156.7 1.3 fusion.109
  158.0 0.5 copy-done.8
  158.5 1.3 fusion.110
  159.9 6.0 %fusion.72 = bf16[56,64,1792]{2,1,0:T(8,128)(2,1)} fusion(f32[56,64,256]{2,1,0:T(8,128)S(1)} %fusion.117, f32[56,256]{1,0:T(8,128)S(1)} %copy-done.49, f32[56]{0:T(128)S(1)} %copy-done.54, f32[56,256]{1,0:T(8,128)S(1)} %copy-done.50, f32[56,256]{1,0:T(8,128)S(1)} %copy-done.34, f32[256,256]{1,0:T(8,128)S(1)} %copy-done.22, ...), kind=kOutput, calls=%fused_computation.109 | convolution fusion | flops 497287168 | bytes 9732608 | tf_op jit(solution)/shard_map/hij,hpj->hpi/dot_general | solution.py:27
  165.9 6.0 %fusion.73 = bf16[56,64,1792]{2,1,0:T(8,128)(2,1)} fusion(bf16[56,64,1792]{2,1,0:T(8,128)(2,1)} %fusion.72, f32[56,64,256]{2,1,0:T(8,128)S(1)} %fusion.105, f32[56,256]{1,0:T(8,128)S(1)} %copy-done.40, f32[56]{0:T(128)S(1)} %copy-done.54, f32[56,256]{1,0:T(8,128)S(1)} %copy-done.41, f32[56,256]{1,0:T(8,128)S(1)} %copy-done.24, ...), kind=kOutput, calls=%fused_computation.110 | convolution fusion | flops 497287168 | bytes 9732608 | tf_op jit(solution)/shard_map/hij,hpj->hpi/dot_general | solution.py:27
  172.0 6.2 %fusion.74 = bf16[56,64,1792]{2,1,0:T(8,128)(2,1)} fusion(bf16[56,64,1792]{2,1,0:T(8,128)(2,1)} %fusion.73, f32[56,64,256]{2,1,0:T(8,128)S(1)} %fusion.106, f32[56,256]{1,0:T(8,128)S(1)} %copy-done.38, f32[56]{0:T(128)S(1)} %copy-done.54, f32[56,256]{1,0:T(8,128)S(1)} %copy-done.39, f32[56,256]{1,0:T(8,128)S(1)} %get-tuple-element.50, ...), kind=kOutput, calls=%fused_computation.111 | convolution fusion | flops 497287168 | bytes 9732608 | tf_op jit(solution)/shard_map/hij,hpj->hpi/dot_general | solution.py:27
  178.3 6.0 %fusion.75 = bf16[56,64,1792]{2,1,0:T(8,128)(2,1)} fusion(bf16[56,64,1792]{2,1,0:T(8,128)(2,1)} %fusion.74, f32[56,64,256]{2,1,0:T(8,128)S(1)} %fusion.107, f32[56,256]{1,0:T(8,128)S(1)} %copy-done.37, f32[56]{0:T(128)S(1)} %copy-done.54, f32[56,256]{1,0:T(8,128)S(1)} %copy-done.48, f32[56,256]{1,0:T(8,128)S(1)} %copy-done.32, ...), kind=kOutput, calls=%fused_computation.112 | convolution fusion | flops 497287168 | bytes 9732608 | tf_op jit(solution)/shard_map/hij,hpj->hpi/dot_general | solution.py:27
  184.3 6.0 %fusion.76 = bf16[56,64,1792]{2,1,0:T(8,128)(2,1)} fusion(bf16[56,64,1792]{2,1,0:T(8,128)(2,1)} %fusion.75, f32[56,64,256]{2,1,0:T(8,128)S(1)} %fusion.108, f32[56,256]{1,0:T(8,128)S(1)} %copy-done.46, f32[56]{0:T(128)S(1)} %copy-done.54, f32[56,256]{1,0:T(8,128)S(1)} %copy-done.47, f32[56,256]{1,0:T(8,128)S(1)} %copy-done.30, ...), kind=kOutput, calls=%fused_computation.113 | convolution fusion | flops 497287168 | bytes 9732608 | tf_op jit(solution)/shard_map/hij,hpj->hpi/dot_general | solution.py:27
  190.3 6.0 %fusion.77 = bf16[56,64,1792]{2,1,0:T(8,128)(2,1)} fusion(bf16[56,64,1792]{2,1,0:T(8,128)(2,1)} %fusion.76, f32[56,64,256]{2,1,0:T(8,128)S(1)} %fusion.109, f32[56,256]{1,0:T(8,128)S(1)} %copy-done.44, f32[56]{0:T(128)S(1)} %copy-done.54, f32[56,256]{1,0:T(8,128)S(1)} %copy-done.45, f32[56,256]{1,0:T(8,128)S(1)} %copy-done.28, ...), kind=kOutput, calls=%fused_computation.114 | convolution fusion | flops 497287168 | bytes 9732608 | tf_op jit(solution)/shard_map/hij,hpj->hpi/dot_general | solution.py:27
  196.4 5.9 %fusion.78 = bf16[56,64,1792]{2,1,0:T(8,128)(2,1)} fusion(bf16[56,64,1792]{2,1,0:T(8,128)(2,1)} %fusion.77, f32[56,64,256]{2,1,0:T(8,128)S(1)} %fusion.110, f32[56,256]{1,0:T(8,128)S(1)} %copy-done.42, f32[56]{0:T(128)S(1)} %copy-done.54, f32[56,256]{1,0:T(8,128)S(1)} %copy-done.43, f32[56,256]{1,0:T(8,128)S(1)} %copy-done.26, ...), kind=kOutput, calls=%fused_computation.115 | convolution fusion | flops 497287168 | bytes 9732608 | tf_op jit(solution)/shard_map/hij,hpj->hpi/dot_general | solution.py:27
  (180 shorter events, 8.0 us)
Async XLA Ops:
  0.0 11.6 %copy-start.16 = (f32[56,1792]{1,0:T(8,128)S(1)}, f32[56,1792]{1,0:T(8,128)}, u32[]{:S(2)}) copy-start(f32[56,1792]{1,0:T(8,128)} %param.9) | copy-start | bytes 1204228
  1.9 19.2 %collective-permute-start = (bf16[3584,3]{0,1:T(4,128)(2,1)S(1)}, bf16[3584,3]{0,1:T(4,128)(2,1)S(1)}, u32[]{:S(2)}, u32[]{:S(2)}) collective-permute-start(bf16[3584,3]{0,1:T(4,128)(2,1)S(1)} %copy.125), channel_id=1, source_target_pairs={{0,1},{1,2},{2,3},{3,4},{4,5},{5,6},{6,7},{7,8},{8,9},{9,10},{10,1... | collective-permute-start | bytes 64520 | tf_op jit(solution)/shard_map/ppermute | solution.py:12
  6.8 13.2 %copy-start.11 = (bf16[128,1792]{1,0:T(8,128)(2,1)S(1)}, bf16[128,1792]{1,0:T(8,128)(2,1)}, u32[]{:S(2)}) copy-start(bf16[128,1792]{1,0:T(8,128)(2,1)} %param.8) | copy-start | bytes 1376260
  11.0 9.9 %copy-start.36 = (f32[4,3584]{1,0:T(4,128)S(1)}, f32[4,3584]{1,0:T(4,128)}, u32[]{:S(2)}) copy-start(f32[4,3584]{1,0:T(4,128)} %param.11) | copy-start | bytes 172036
  11.4 10.1 %copy-start.51 = (f32[3584]{0:T(1024)S(1)}, f32[3584]{0:T(1024)}, u32[]{:S(2)}) copy-start(f32[3584]{0:T(1024)} %param.12) | copy-start | bytes 43012
  12.1 7.9 %copy-start.23 = (f32[56,256]{1,0:T(8,128)}, f32[56,256]{1,0:T(8,128)S(1)}, u32[]{:S(2)}) copy-start(f32[56,256]{1,0:T(8,128)S(1)} %get-tuple-element.51) | copy-start | bytes 172036
  13.0 7.0 %copy-start.25 = (f32[56,256]{1,0:T(8,128)}, f32[56,256]{1,0:T(8,128)S(1)}, u32[]{:S(2)}) copy-start(f32[56,256]{1,0:T(8,128)S(1)} %get-tuple-element.48) | copy-start | bytes 172036
  13.0 49.8 %copy-start.27 = (f32[56,256]{1,0:T(8,128)}, f32[56,256]{1,0:T(8,128)S(1)}, u32[]{:S(2)}) copy-start(f32[56,256]{1,0:T(8,128)S(1)} %get-tuple-element.47) | copy-start | bytes 172036
  13.0 49.8 %copy-start.29 = (f32[56,256]{1,0:T(8,128)}, f32[56,256]{1,0:T(8,128)S(1)}, u32[]{:S(2)}) copy-start(f32[56,256]{1,0:T(8,128)S(1)} %get-tuple-element.46) | copy-start | bytes 172036
  13.0 49.8 %copy-start.31 = (f32[56,256]{1,0:T(8,128)}, f32[56,256]{1,0:T(8,128)S(1)}, u32[]{:S(2)}) copy-start(f32[56,256]{1,0:T(8,128)S(1)} %get-tuple-element.45) | copy-start | bytes 172036
  13.0 49.8 %copy-start.33 = (f32[56,256]{1,0:T(8,128)}, f32[56,256]{1,0:T(8,128)S(1)}, u32[]{:S(2)}) copy-start(f32[56,256]{1,0:T(8,128)S(1)} %get-tuple-element.49) | copy-start | bytes 172036
  15.3 62.2 %all-to-all-start.1 = ((f32[32,1,112]{2,1,0:T(1,128)}), f32[32,1,112]{2,1,0:T(1,128)S(1)}, u32[]{:S(2)}, u32[]{:S(2)}) async-start(f32[32,1,112]{2,1,0:T(1,128)} %all_to_all.24), calls=%async_computation.1 | async-start | bytes 32768 | tf_op jit(solution)/shard_map/all_to_all | solution.py:99
  62.9 8.5 %copy-start = (bf16[3584,1792]{1,0:T(8,128)(2,1)S(1)}, bf16[3584,1792]{1,0:T(8,128)(2,1)}, u32[]{:S(2)}) copy-start(bf16[3584,1792]{1,0:T(8,128)(2,1)} %multiply_convert_fusion) | copy-start | bytes 38535172
  65.2 3.4 %copy-start.14 = (f32[56,64,64]{2,1,0:T(8,128)}, f32[56,64,64]{2,1,0:T(8,128)S(1)}, u32[]{:S(2)}) copy-start(f32[56,64,64]{2,1,0:T(8,128)S(1)} %fusion.51) | copy-start | bytes 2752516
  68.5 2.9 %copy-start.9 = (f32[56,64,64]{2,1,0:T(8,128)}, f32[56,64,64]{2,1,0:T(8,128)S(1)}, u32[]{:S(2)}) copy-start(f32[56,64,64]{2,1,0:T(8,128)S(1)} %multiply_add_fusion.5) | copy-start | bytes 2752516
  71.4 1.3 copy-start.1
  72.1 1.3 copy-start.3
  72.7 1.2 copy-start.5
  73.4 1.3 copy-start.7
  77.4 27.1 %all-to-all-start = ((f32[32,1,7168]{2,1,0:T(1,128)}), f32[32,1,7168]{2,1,0:T(1,128)}, u32[]{:S(2)}, u32[]{:S(2)}) async-start(f32[32,1,7168]{2,1,0:T(1,128)} %all_to_all.30), calls=%async_computation | async-start | bytes 1835008 | tf_op jit(solution)/shard_map/all_to_all | solution.py:98
  87.6 21.6 %copy-start.12 = (f32[16,7168]{1,0:T(8,128)S(1)}, f32[16,7168]{1,0:T(8,128)}, u32[]{:S(2)}) copy-start(f32[16,7168]{1,0:T(8,128)} %slice.389) | copy-start | bytes 1376260
  87.6 21.6 %copy-start.13 = (f32[16,7168]{1,0:T(8,128)S(1)}, f32[16,7168]{1,0:T(8,128)}, u32[]{:S(2)}) copy-start(f32[16,7168]{1,0:T(8,128)} %slice.385) | copy-start | bytes 1376260
  119.0 27.0 %all-to-all-start.2 = ((f32[32,1,7168]{2,1,0:T(1,128)}), f32[32,1,7168]{2,1,0:T(1,128)S(1)}, u32[]{:S(2)}, u32[]{:S(2)}) async-start(f32[32,1,7168]{2,1,0:T(1,128)} %copy.108), calls=%async_computation.2 | async-start | bytes 1835008 | tf_op jit(solution)/shard_map/all_to_all | solution.py:104
  148.7 1.5 copy-start.15
  150.2 1.5 copy-start.10
  150.2 1.5 copy-start.53
  151.7 1.5 copy-start.2
  151.7 1.5 copy-start.52
  151.7 8.1 %slice-start = ((s8[12845056]{0:T(1024)(128)(4,1)}), s8[4194304]{0:T(1024)(128)(4,1)S(1)}, s32[]{:S(2)}) async-start(s8[12845056]{0:T(1024)(128)(4,1)} %bitcast.100), calls=%async_computation.3 | async-start | bytes 8388608
  153.2 1.8 copy-start.4
  153.2 6.6 %slice-start.1 = ((s8[12845056]{0:T(1024)(128)(4,1)}), s8[4194304]{0:T(1024)(128)(4,1)S(1)}, s32[]{:S(2)}) async-start(s8[12845056]{0:T(1024)(128)(4,1)} %bitcast.100), calls=%async_computation.4 | async-start | bytes 8388608
  155.0 1.7 copy-start.6
  155.0 4.8 %slice-start.2 = ((s8[12845056]{0:T(1024)(128)(4,1)}), s8[4194304]{0:T(1024)(128)(4,1)S(1)}, s32[]{:S(2)}) async-start(s8[12845056]{0:T(1024)(128)(4,1)} %bitcast.100), calls=%async_computation.5 | async-start | bytes 8388608
  156.7 1.7 copy-start.8
  156.7 3.1 %slice-start.3 = ((s8[12845056]{0:T(1024)(128)(4,1)}), s8[262144]{0:T(1024)(128)(4,1)S(1)}, s32[]{:S(2)}) async-start(s8[12845056]{0:T(1024)(128)(4,1)} %bitcast.100), calls=%async_computation.6 | async-start | bytes 524288
  158.5 1.3 copy-start.22
  158.5 1.4 copy-start.34
  158.5 1.4 copy-start.35
  158.5 1.4 copy-start.49
  158.5 1.4 copy-start.50
  158.5 1.4 copy-start.54
  159.9 6.0 %copy-start.21 = (f32[256,256]{1,0:T(8,128)S(1)}, f32[256,256]{1,0:T(8,128)}, u32[]{:S(2)}) copy-start(f32[256,256]{1,0:T(8,128)} %fusion.146) | copy-start | bytes 786436
  159.9 6.0 %copy-start.24 = (f32[56,256]{1,0:T(8,128)S(1)}, f32[56,256]{1,0:T(8,128)}, u32[]{:S(2)}) copy-start(f32[56,256]{1,0:T(8,128)} %copy-done.23) | copy-start | bytes 172036
  159.9 6.0 %copy-start.40 = (f32[56,256]{1,0:T(8,128)S(1)}, f32[56,256]{1,0:T(8,128)}, u32[]{:S(2)}) copy-start(f32[56,256]{1,0:T(8,128)} %get-tuple-element.44) | copy-start | bytes 172036
  159.9 6.0 %copy-start.41 = (f32[56,256]{1,0:T(8,128)S(1)}, f32[56,256]{1,0:T(8,128)}, u32[]{:S(2)}) copy-start(f32[56,256]{1,0:T(8,128)} %get-tuple-element.58) | copy-start | bytes 172036
  165.9 6.1 %copy-start.20 = (f32[256,256]{1,0:T(8,128)S(1)}, f32[256,256]{1,0:T(8,128)}, u32[]{:S(2)}) copy-start(f32[256,256]{1,0:T(8,128)} %fusion.143) | copy-start | bytes 786436
  165.9 6.0 %copy-start.38 = (f32[56,256]{1,0:T(8,128)S(1)}, f32[56,256]{1,0:T(8,128)}, u32[]{:S(2)}) copy-start(f32[56,256]{1,0:T(8,128)} %get-tuple-element.42) | copy-start | bytes 172036
  165.9 6.0 %copy-start.39 = (f32[56,256]{1,0:T(8,128)S(1)}, f32[56,256]{1,0:T(8,128)}, u32[]{:S(2)}) copy-start(f32[56,256]{1,0:T(8,128)} %get-tuple-element.59) | copy-start | bytes 172036
  172.0 6.3 %copy-start.19 = (f32[256,256]{1,0:T(8,128)S(1)}, f32[256,256]{1,0:T(8,128)}, u32[]{:S(2)}) copy-start(f32[256,256]{1,0:T(8,128)} %fusion.140) | copy-start | bytes 786436
  172.0 6.3 %copy-start.32 = (f32[56,256]{1,0:T(8,128)S(1)}, f32[56,256]{1,0:T(8,128)}, u32[]{:S(2)}) copy-start(f32[56,256]{1,0:T(8,128)} %copy-done.31) | copy-start | bytes 172036
  172.0 6.3 %copy-start.37 = (f32[56,256]{1,0:T(8,128)S(1)}, f32[56,256]{1,0:T(8,128)}, u32[]{:S(2)}) copy-start(f32[56,256]{1,0:T(8,128)} %get-tuple-element.40) | copy-start | bytes 172036
  172.0 6.2 %copy-start.48 = (f32[56,256]{1,0:T(8,128)S(1)}, f32[56,256]{1,0:T(8,128)}, u32[]{:S(2)}) copy-start(f32[56,256]{1,0:T(8,128)} %get-tuple-element.60) | copy-start | bytes 172036
  178.2 6.0 %copy-start.18 = (f32[256,256]{1,0:T(8,128)S(1)}, f32[256,256]{1,0:T(8,128)}, u32[]{:S(2)}) copy-start(f32[256,256]{1,0:T(8,128)} %fusion.137) | copy-start | bytes 786436
  178.3 6.0 %copy-start.30 = (f32[56,256]{1,0:T(8,128)S(1)}, f32[56,256]{1,0:T(8,128)}, u32[]{:S(2)}) copy-start(f32[56,256]{1,0:T(8,128)} %copy-done.29) | copy-start | bytes 172036
  178.3 6.0 %copy-start.46 = (f32[56,256]{1,0:T(8,128)S(1)}, f32[56,256]{1,0:T(8,128)}, u32[]{:S(2)}) copy-start(f32[56,256]{1,0:T(8,128)} %get-tuple-element.38) | copy-start | bytes 172036
  178.3 6.0 %copy-start.47 = (f32[56,256]{1,0:T(8,128)S(1)}, f32[56,256]{1,0:T(8,128)}, u32[]{:S(2)}) copy-start(f32[56,256]{1,0:T(8,128)} %get-tuple-element.61) | copy-start | bytes 172036
  184.3 6.0 %copy-start.17 = (f32[256,256]{1,0:T(8,128)S(1)}, f32[256,256]{1,0:T(8,128)}, u32[]{:S(2)}) copy-start(f32[256,256]{1,0:T(8,128)} %fusion.134) | copy-start | bytes 786436
  184.3 6.0 %copy-start.28 = (f32[56,256]{1,0:T(8,128)S(1)}, f32[56,256]{1,0:T(8,128)}, u32[]{:S(2)}) copy-start(f32[56,256]{1,0:T(8,128)} %copy-done.27) | copy-start | bytes 172036
  184.3 6.0 %copy-start.44 = (f32[56,256]{1,0:T(8,128)S(1)}, f32[56,256]{1,0:T(8,128)}, u32[]{:S(2)}) copy-start(f32[56,256]{1,0:T(8,128)} %get-tuple-element.36) | copy-start | bytes 172036
  184.3 6.0 %copy-start.45 = (f32[56,256]{1,0:T(8,128)S(1)}, f32[56,256]{1,0:T(8,128)}, u32[]{:S(2)}) copy-start(f32[56,256]{1,0:T(8,128)} %get-tuple-element.62) | copy-start | bytes 172036
  190.3 6.1 %copy-start.26 = (f32[56,256]{1,0:T(8,128)S(1)}, f32[56,256]{1,0:T(8,128)}, u32[]{:S(2)}) copy-start(f32[56,256]{1,0:T(8,128)} %copy-done.25) | copy-start | bytes 172036
  190.3 6.0 %copy-start.42 = (f32[56,256]{1,0:T(8,128)S(1)}, f32[56,256]{1,0:T(8,128)}, u32[]{:S(2)}) copy-start(f32[56,256]{1,0:T(8,128)} %get-tuple-element.31) | copy-start | bytes 172036
  190.3 6.0 %copy-start.43 = (f32[56,256]{1,0:T(8,128)S(1)}, f32[56,256]{1,0:T(8,128)}, u32[]{:S(2)}) copy-start(f32[56,256]{1,0:T(8,128)} %get-tuple-element.63) | copy-start | bytes 172036
where the time goes:
time: 206 us; the launch traced here: 202 us
  matrix products  67.2 us (33%)
  other arithmetic  53.9 us (26%)
  waiting for transfers between devices  31.8 us (15%)
  local copies, waits for them, and re-layouts  28.2 us (14%)
  starting transfers between devices  20 us (10%)
    dot_general x7, matrix products, block_local(): jnp.einsum('hij,hpj->hpi', weights, block_inputs, preferred_element_type=...  42.1 us
    convert_element_type x1, other arithmetic, local(): values = jax.nn.silu(convolved).astype(jnp.bfloat16)  41.3 us
    all_to_all x1, waiting for transfers between devices, local(): lax.all_to_all(send_state, 'cp', split_axis=0, concat_axis=0, tiled=True)  16.9 us
    all_to_all x1, waiting for transfers between devices, local(): lax.all_to_all(before_state, 'cp', split_axis=0, concat_axis=0, tiled=True)  14.8 us
    dot_general x7, matrix products, local(): jnp.einsum('hnj,hpj->hnp', scaled, piece_in, preferred_element_type=jnp.f...  11 us
    slice x25, local copies, waits for them, and re-layouts, local(): lax.associative_scan(merge_rows, (wide_decay, got_state), axis=0)  10.2 us
    dot_general x7, matrix products, block_carried(): jnp.einsum('hnp,ni->hpi', block_entering, query_rows, preferred_element_t...  8.42 us
    all_to_all x1, starting transfers between devices, local(): lax.all_to_all(send_state, 'cp', split_axis=0, concat_axis=0, tiled=True)  5.89 us
  transfers between devices with their start and end apart: 4, of which 2 were waited for; matrix products, arithmetic and copies ran while one was open for 36% of the time, Pallas kernels for 0%

commit v1 on v0

v1 whole, which is shorter than its diff:
```python
import functools

import jax
import jax.numpy as jnp
from jax import lax
from jax.experimental import pallas as pl
from jax.experimental.pallas import tpu as pltpu
from jax.sharding import PartitionSpec as P

HALF = 64
TILE = 128
PAIR = 256
GROUP = 8


def prepare_kernel(state_dim, decay_ref, step_ref, maps_ref, e_ref, b_ref, a0_ref, a1_ref, f_ref, d_ref,
                   total_ref, key_ref, mix_ref):
    tiles = decay_ref.shape[1] // TILE
    heads = decay_ref.shape[0]
    row = lax.broadcasted_iota(jnp.int32, (TILE, TILE), 0)
    col = lax.broadcasted_iota(jnp.int32, (TILE, TILE), 1)
    upper = (row <= col).astype(jnp.float32)
    same = (row <= col) & ((row < HALF) == (col < HALF))
    cross = (row < HALF) & (col >= HALF)
    lane = lax.broadcasted_iota(jnp.int32, (heads, TILE), 1)
    low_cols = lax.broadcasted_iota(jnp.int32, (state_dim, TILE), 1) < HALF
    total = jnp.zeros((heads, TILE), jnp.float32)
    for t in range(tiles):
        span = slice(t * TILE, (t + 1) * TILE)
        sums = jnp.dot(decay_ref[:, span], upper, precision=lax.Precision.HIGHEST,
                       preferred_element_type=jnp.float32)
        step = step_ref[:, span]
        first = jnp.broadcast_to(sums[:, HALF // 2 - 1:HALF // 2], (heads, TILE))
        second = jnp.broadcast_to(sums[:, HALF + HALF // 2 - 1:HALF + HALF // 2], (heads, TILE))
        end = jnp.broadcast_to(sums[:, TILE - 1:], (heads, TILE))
        middle = jnp.where(lane < HALF, first, second)
        e_ref[:, span] = jnp.exp(end - sums) * step
        b_ref[:, span] = jnp.exp(middle - sums) * step
        a0_ref[:, span] = jnp.exp(sums - middle)
        a1_ref[:, span] = jnp.where(lane < HALF, 0.0, jnp.exp(jnp.where(lane < HALF, 0.0, sums - first)))
        f_ref[:, span] = jnp.exp(first)
        d_ref[:, span] = jnp.exp(end)
        total = total + end
        keys = maps_ref[:state_dim, span]
        queries = maps_ref[state_dim:, span]
        keys_t = keys.astype(jnp.float32).T.astype(jnp.bfloat16)
        affinity = jnp.dot(keys_t, queries, preferred_element_type=jnp.float32)
        zero_keys = jnp.zeros_like(keys_t)
        side = [keys_t, zero_keys] if t % 2 == 0 else [zero_keys, keys_t]
        key_ref[t // 2, (t % 2) * TILE:(t % 2 + 1) * TILE, :] = jnp.concatenate(side, axis=1)
        mix_ref[t, :TILE, :TILE] = jnp.where(same, affinity, 0.0).astype(jnp.bfloat16)
        mix_ref[t, :TILE, TILE:] = jnp.where(cross, affinity, 0.0).astype(jnp.bfloat16)
        wide = queries.astype(jnp.float32)
        mix_ref[t, TILE:, :TILE] = jnp.where(low_cols, wide, 0.0).astype(jnp.bfloat16)
        mix_ref[t, TILE:, TILE:] = jnp.where(low_cols, 0.0, wide).astype(jnp.bfloat16)
    total_ref[...] = total


def rows_of(vector, head_dim):
    count, width = vector.shape
    return jnp.broadcast_to(vector[:, None, :], (count, head_dim, width)).reshape(count * head_dim, width)


def state_kernel(head_dim, state_dim, raw_ref, side_ref, e_ref, d_ref, total_ref, key_ref, x_ref, part_ref,
                 message_ref, column_ref, scaled_ref, spread_ref):
    rows, tokens = raw_ref.shape
    tiles = tokens // TILE
    side = side_ref[...]
    padded = jnp.concatenate([jnp.zeros((TILE - side.shape[0], rows), jnp.float32), side], axis=0)
    column_ref[...] = padded.T
    spread_ref[...] = rows_of(e_ref[...], 8)
    step_rows = head_dim // 2
    base = TILE - side.shape[0]

    def convolve(group, carry):
        start = pl.multiple_of(group * step_rows, step_rows)
        head = group // 2
        lane = lax.broadcasted_iota(jnp.int32, (step_rows, TILE), 1)
        columns = column_ref[pl.ds(start, step_rows), :]
        w0, w1, w2, w3, bias = [
            jnp.broadcast_to(columns[:, base + k:base + k + 1], (step_rows, TILE)) for k in range(5)
        ]
        before1 = pltpu.roll(columns, 1, 1)
        before2 = pltpu.roll(w1 * columns + w0 * before1, 2, 1)
        for t in range(tiles):
            span = slice(t * TILE, (t + 1) * TILE)
            now = raw_ref[pl.ds(start, step_rows), span].astype(jnp.float32)
            turned = pltpu.roll(now, 1, 1)
            late1 = jnp.where(lane < 1, before1, turned)
            before1 = turned
            turned = pltpu.roll(w1 * now + w0 * late1, 2, 1)
            late2 = jnp.where(lane < 2, before2, turned)
            before2 = turned
            half = (bias + w3 * now) + (w2 * late1 + late2)
            value = half + half * jnp.tanh(half)
            weight = jnp.concatenate([spread_ref[pl.ds(pl.multiple_of(head * 8, 8), 8), span]] * (step_rows // 8), axis=0)
            x_ref[pl.ds(start, step_rows), span] = value.astype(jnp.bfloat16)
            scaled_ref[pl.ds(start, step_rows), span] = (value * weight).astype(jnp.bfloat16)
        return carry

    lax.fori_loop(0, rows // step_rows, convolve, 0)
    state = jnp.zeros((rows, state_dim), jnp.float32)
    for k in range(tokens // PAIR):
        part = jnp.dot(scaled_ref[:, k * PAIR:(k + 1) * PAIR], key_ref[k], preferred_element_type=jnp.float32)
        part_ref[:, k * TILE:(k + 1) * TILE] = part.astype(jnp.bfloat16)
        for i in range(2):
            decay = rows_of(d_ref[:, (2 * k + i) * TILE:(2 * k + i) * TILE + state_dim], head_dim)
            state = decay * state + part[:, i * state_dim:(i + 1) * state_dim]
    total = rows_of(total_ref[:, :state_dim], head_dim)
    high = total.astype(jnp.bfloat16)
    rest = total - high.astype(jnp.float32)
    middle = rest.astype(jnp.bfloat16)
    low = rest - middle.astype(jnp.float32)
    lane = lax.broadcasted_iota(jnp.int32, (rows, state_dim), 1)
    logs = jnp.where(lane == 0, high.astype(jnp.float32), jnp.where(lane == 1, middle.astype(jnp.float32), low))
    message_ref[...] = jnp.concatenate([state, logs], axis=1).astype(jnp.bfloat16)


def combine_kernel(state_dim, got_ref, out_ref):
    peers, rows, width = got_ref.shape
    running = jnp.zeros((rows, width), jnp.float32)
    for d in range(peers):
        out_ref[d] = running.astype(jnp.bfloat16)
        got = got_ref[d].astype(jnp.float32)
        log = (got[:, state_dim:state_dim + 1] + got[:, state_dim + 1:state_dim + 2]) + got[:, state_dim + 2:state_dim + 3]
        running = jnp.exp(log) * running + got


def output_kernel(head_dim, state_dim, x_ref, part_ref, enter_ref, b_ref, a0_ref, a1_ref, f_ref, d_ref, gain_ref,
                  mix_ref, out_ref, state_ref):
    tokens = x_ref.shape[1]
    state_ref[...] = enter_ref[:, :state_dim].astype(jnp.float32)
    gain = rows_of(gain_ref[...], head_dim)

    def pair(k, carry):
        parts = part_ref[:, pl.ds(pl.multiple_of(k * TILE, TILE), TILE)].astype(jnp.float32)
        for i in range(2):
            span = pl.ds(pl.multiple_of(k * PAIR + i * TILE, TILE), TILE)
            x = x_ref[:, span].astype(jnp.float32)
            scaled = (x * rows_of(b_ref[:, span], head_dim)).astype(jnp.bfloat16)
            state = state_ref[...]
            entering = (state * rows_of(f_ref[:, span], head_dim)[:, :state_dim]).astype(jnp.bfloat16)
            left = jnp.concatenate([scaled, entering], axis=1)
            mixed = jnp.dot(left, mix_ref[2 * k + i], preferred_element_type=jnp.float32)
            out = mixed[:, :TILE] * rows_of(a0_ref[:, span], head_dim)
            out = out + mixed[:, TILE:] * rows_of(a1_ref[:, span], head_dim)
            out_ref[:, span] = (out + gain * x).astype(jnp.bfloat16)
            state_ref[...] = state * rows_of(d_ref[:, span], head_dim)[:, :state_dim] + parts[
                :, i * state_dim:(i + 1) * state_dim]
        return carry

    lax.fori_loop(0, tokens // PAIR, pair, 0)


def local(raw_inputs, state_maps, step_size, log_decay, conv_weight, conv_bias, skip_gain):
    taps = conv_weight.shape[0]
    channels, tokens = raw_inputs.shape
    heads = skip_gain.shape[0]
    head_dim = channels // heads
    state_dim = state_maps.shape[0] // 2
    peers = lax.axis_size("cp")
    tiles = tokens // TILE
    group_rows = GROUP * head_dim
    f32, bf16 = jnp.float32, jnp.bfloat16

    tail = raw_inputs[:, tokens - (taps - 1):].T
    halo = lax.ppermute(tail, "cp", [(s, s + 1) for s in range(peers - 1)])
    vector = jax.ShapeDtypeStruct((heads, tokens), f32)
    e, b, a0, a1, f, d, total, keys, mix = pl.pallas_call(
        functools.partial(prepare_kernel, state_dim),
        out_shape=[vector] * 6 + [
            jax.ShapeDtypeStruct((heads, TILE), f32),
            jax.ShapeDtypeStruct((tiles // 2, PAIR, 2 * state_dim), bf16),
            jax.ShapeDtypeStruct((tiles, TILE + state_dim, 2 * TILE), bf16),
        ],
        cost_estimate=pl.CostEstimate(flops=100000000, bytes_accessed=6000000, transcendentals=0),
    )(log_decay, step_size, state_maps)
    side = jnp.concatenate([0.5 * conv_weight, 0.5 * conv_bias[None], halo.astype(f32)], axis=0)

    grid = heads // GROUP
    wide = lambda cols: pl.BlockSpec((group_rows, cols), lambda g: (g, 0))
    vec = pl.BlockSpec((GROUP, tokens), lambda g: (g, 0))
    vec1 = pl.BlockSpec((GROUP, TILE), lambda g: (g, 0))
    full = lambda array: pl.BlockSpec(array.shape, lambda g: (0,) * array.ndim)
    x, part, message = pl.pallas_call(
        functools.partial(state_kernel, head_dim, state_dim),
        grid=(grid,),
        in_specs=[wide(tokens), pl.BlockSpec((side.shape[0], group_rows), lambda g: (0, g)), vec, vec, vec1, full(keys)],
        out_specs=[wide(tokens), wide(tiles * state_dim), wide(2 * state_dim)],
        out_shape=[
            jax.ShapeDtypeStruct((channels, tokens), bf16),
            jax.ShapeDtypeStruct((channels, tiles * state_dim), bf16),
            jax.ShapeDtypeStruct((channels, 2 * state_dim), bf16),
        ],
        scratch_shapes=[pltpu.VMEM((group_rows, TILE), f32), pltpu.VMEM((group_rows, tokens), bf16),
                        pltpu.VMEM((GROUP * 8, tokens), f32)],
        compiler_params=pltpu.CompilerParams(dimension_semantics=("arbitrary",)),
    )(raw_inputs, side, e, d, total, keys)

    send = message.reshape(peers, channels // peers, 2 * state_dim)
    got = lax.all_to_all(send, "cp", split_axis=0, concat_axis=0, tiled=True)
    before = pl.pallas_call(
        functools.partial(combine_kernel, state_dim),
        out_shape=jax.ShapeDtypeStruct(got.shape, bf16),
    )(got)
    returned = lax.all_to_all(before, "cp", split_axis=0, concat_axis=0, tiled=True)
    enter = returned.reshape(channels, 2 * state_dim)
    gain = jnp.broadcast_to(skip_gain[:, None], (heads, TILE))
    return pl.pallas_call(
        functools.partial(output_kernel, head_dim, state_dim),
        grid=(grid,),
        in_specs=[wide(tokens), wide(tiles * state_dim), wide(2 * state_dim), vec, vec, vec, vec, vec, vec1, full(mix)],
        out_specs=wide(tokens),
        out_shape=jax.ShapeDtypeStruct((channels, tokens), bf16),
        scratch_shapes=[pltpu.VMEM((group_rows, state_dim), f32)],
        compiler_params=pltpu.CompilerParams(dimension_semantics=("arbitrary",)),
    )(x, part, enter, b, a0, a1, f, d, gain, mix)


def solution(mesh):
    placed = (P(None, "cp"), P(None, "cp"), P(None, "cp"), P(None, "cp"), P(), P(), P())
    return jax.shard_map(
        local, mesh=mesh, in_specs=placed, out_specs=P(None, "cp"), check_vma=False
    )
```

time: 206 us -> 137 us (0.67)
  the two profiles are of different devices: /device:TPU:29 before, /device:TPU:0 now
where the time goes in v1:
time: 137 us
  Pallas kernels  71.6 us (52%)
  blocking collectives  57.8 us (42%)
  local copies, waits for them, and re-layouts  2.56 us (2%)
  starting transfers between devices  2.4 us (2%)
  other arithmetic  2.27 us (2%)
    pallas_call x1, Pallas kernels, local(): pl.pallas_call(functools.partial(state_kernel, head_dim, state_dim), grid...  40.8 us
    all_to_all x1, blocking collectives, local(): got = lax.all_to_all(send, 'cp', split_axis=0, concat_axis=0, tiled=True)  30.6 us
    all_to_all x1, blocking collectives, local(): lax.all_to_all(before, 'cp', split_axis=0, concat_axis=0, tiled=True)  27.1 us
    pallas_call x1, Pallas kernels, local(): pl.pallas_call(functools.partial(output_kernel, head_dim, state_dim), gri...  21.2 us
    pallas_call x1, Pallas kernels, local(): pl.pallas_call(functools.partial(combine_kernel, state_dim), out_shape=ja...  5 us
    pallas_call x1, Pallas kernels, local(): pl.pallas_call(functools.partial(prepare_kernel, state_dim), out_shape=[v...  4.51 us
  transfers between devices with their start and end apart: 1, of which 0 were waited for; matrix products, arithmetic and copies ran while one was open for 1% of the time, Pallas kernels for 3%

profile of v1, /device:TPU:0, one launch (start us, length us, event | category | flops | bytes accessed | tf_op | source)
XLA Modules:
  0.0 136.6 jit_solution(4781659087755804615)
XLA Ops:
  0.0 0.0 copy-start
  0.0 1.5 %slice.3 = bf16[3584,3]{1,0:T(8,128)(2,1)S(1)} slice(bf16[3584,1792]{1,0:T(8,128)(2,1)} %raw_ref.1), slice={[0:3584], [1789:1792]} | slice | bytes 43008 | tf_op jit(solution)/shard_map/slice | solution.py:166
  1.5 0.3 copy.9
  1.9 2.4 %collective-permute-start = (bf16[3,3584]{1,0:T(4,128)(2,1)S(1)}, bf16[3,3584]{1,0:T(4,128)(2,1)S(1)}, u32[]{:S(2)}, u32[]{:S(2)}) collective-permute-start(bf16[3,3584]{1,0:T(4,128)(2,1)S(1)} %bitcast.5), channel_id=1, source_target_pairs={{0,1},{1,2},{2,3},{3,4},{4,5},{5,6},{6,7},{7,8},{8,9},{9,10},{10,1... | collective-permute-start | bytes 64520 | tf_op jit(solution)/shard_map/ppermute | solution.py:167
  4.3 0.8 broadcast_multiply_fusion
  5.1 0.7 broadcast_multiply_fusion.1
  5.8 4.5 %shard_map.73 = (f32[56,1792]{1,0:T(8,128)}, f32[56,1792]{1,0:T(8,128)}, f32[56,1792]{1,0:T(8,128)}, f32[56,1792]{1,0:T(8,128)}, f32[56,1792]{1,0:T(8,128)}, /*i...) custom-call(f32[56,1792]{1,0:T(8,128)} %decay_ref.1, ...), custom_call_target="tpu_custom_call" | custom-call | flops 100000000 | bytes 6000000 | tf_op jit(solution)/shard_map/pallas_call | solution.py:169
  10.4 0.0 collective-permute-done
  10.4 0.7 pad_maximum_fusion.side_ref
  11.1 40.8 %shard_map.74 = (bf16[3584,1792]{1,0:T(8,128)(2,1)}, bf16[3584,896]{1,0:T(8,128)(2,1)}, bf16[3584,128]{1,0:T(8,128)(2,1)}) custom-call(bf16[3584,1792]{1,0:T(8,128)(2,1)} %raw_ref.1, f32[8,3584]{1,0:T(8,128)} %pad_maximum_fusion.side_ref, f32[56,1792]{1,0:T(8,128)} %get-tuple-element.17.e_ref, f32[56,1792]{1,0:T(8,128)} %get-tuple-element.18.d_ref, ...), custom_call_target="tpu_custom_call" | custom-call | tf_op jit(solution)/shard_map/pallas_call | solution.py:185
  51.9 30.6 %all_to_all.10.got_ref = bf16[32,112,128]{2,1,0:T(8,128)(2,1)} all-to-all(bf16[32,112,128]{2,1,0:T(8,128)(2,1)} %bitcast.4), channel_id=1, replica_groups=mesh['cp'=32] {'cp'}, dimensions={0} | all-to-all | bytes 1835008 | tf_op jit(solution)/shard_map/all_to_all | solution.py:201
  82.5 5.0 %shard_map.75 = bf16[32,112,128]{2,1,0:T(8,128)(2,1)} custom-call(bf16[32,112,128]{2,1,0:T(8,128)(2,1)} %all_to_all.10.got_ref), custom_call_target="tpu_custom_call" | custom-call | tf_op jit(solution)/shard_map/pallas_call | solution.py:202
  87.5 27.1 %all_to_all.11 = bf16[32,112,128]{2,1,0:T(8,128)(2,1)} all-to-all(bf16[32,112,128]{2,1,0:T(8,128)(2,1)} %shard_map.75), channel_id=1, replica_groups=mesh['cp'=32] {'cp'}, dimensions={0} | all-to-all | bytes 1835008 | tf_op jit(solution)/shard_map/all_to_all | solution.py:206
  114.6 0.0 copy-done
  114.6 0.7 broadcast_in_dim.2.gain_ref
  115.3 21.2 %shard_map.76 = bf16[3584,1792]{1,0:T(8,128)(2,1)} custom-call(bf16[3584,1792]{1,0:T(8,128)(2,1)} %get-tuple-element.21.x_ref, bf16[3584,896]{1,0:T(8,128)(2,1)} %get-tuple-element.22.part_ref, bf16[3584,128]{1,0:T(8,128)(2,1)} %bitcast.3, f32[56,1792]{1,0:T(8,128)} %get-tuple-element.24.b_ref, f32[56,1792]{1,0:T(8,128)} %get-tuple-element.25.a0_ref, ...), custom_call_target="tpu_custom_call" | custom-call | tf_op jit(solution)/shard_map/pallas_call | solution.py:209
  (2 shorter events, 0.0 us)
Async XLA Ops:
  0.0 114.6 %copy-start = (f32[56]{0:T(128)S(1)}, f32[56]{0:T(128)}, u32[]{:S(2)}) copy-start(f32[56]{0:T(128)} %param.13) | copy-start | bytes 676
  1.9 8.5 %collective-permute-start = (bf16[3,3584]{1,0:T(4,128)(2,1)S(1)}, bf16[3,3584]{1,0:T(4,128)(2,1)S(1)}, u32[]{:S(2)}, u32[]{:S(2)}) collective-permute-start(bf16[3,3584]{1,0:T(4,128)(2,1)S(1)} %bitcast.5), channel_id=1, source_target_pairs={{0,1},{1,2},{2,3},{3,4},{4,5},{5,6},{6,7},{7,8},{8,9},{9,10},{10,1... | collective-permute-start | bytes 64520 | tf_op jit(solution)/shard_map/ppermute | solution.py:167

commit v2 on v1

--- a/solution.py
+++ b/solution.py
@@ -61,8 +61,8 @@
     return jnp.broadcast_to(vector[:, None, :], (count, head_dim, width)).reshape(count * head_dim, width)
 
 
-def state_kernel(head_dim, state_dim, raw_ref, side_ref, e_ref, d_ref, total_ref, key_ref, x_ref, part_ref,
-                 message_ref, column_ref, scaled_ref, spread_ref):
+def state_kernel(head_dim, state_dim, raw_ref, side_ref, e_ref, d_ref, key_ref, x_ref, part_ref, message_ref,
+                 column_ref, scaled_ref, spread_ref):
     rows, tokens = raw_ref.shape
     tiles = tokens // TILE
     side = side_ref[...]
@@ -106,30 +106,89 @@
         for i in range(2):
             decay = rows_of(d_ref[:, (2 * k + i) * TILE:(2 * k + i) * TILE + state_dim], head_dim)
             state = decay * state + part[:, i * state_dim:(i + 1) * state_dim]
-    total = rows_of(total_ref[:, :state_dim], head_dim)
-    high = total.astype(jnp.bfloat16)
-    rest = total - high.astype(jnp.float32)
-    middle = rest.astype(jnp.bfloat16)
-    low = rest - middle.astype(jnp.float32)
-    lane = lax.broadcasted_iota(jnp.int32, (rows, state_dim), 1)
-    logs = jnp.where(lane == 0, high.astype(jnp.float32), jnp.where(lane == 1, middle.astype(jnp.float32), low))
-    message_ref[...] = jnp.concatenate([state, logs], axis=1).astype(jnp.bfloat16)
-
-
-def combine_kernel(state_dim, got_ref, out_ref):
-    peers, rows, width = got_ref.shape
-    running = jnp.zeros((rows, width), jnp.float32)
+    message_ref[...] = packed(state, head_dim).astype(jnp.bfloat16)
+
+
+def packed(state, head_dim):
+    rows, width = state.shape
+    pieces = state.reshape(rows // head_dim, 2, head_dim // 2, width)
+    return jnp.concatenate([pieces[:, 0], pieces[:, 1]], axis=2).reshape(rows // 2, 2 * width)
+
+
+def unpacked(pairs, head_dim):
+    rows, width = pairs.shape
+    pieces = pairs.reshape(2 * rows // head_dim, head_dim // 2, width)
+    return jnp.concatenate([pieces[:, :, :width // 2], pieces[:, :, width // 2:]], axis=1).reshape(
+        2 * rows, width // 2)
+
+
+def exchange_kernel(peers, own, message_ref, out_ref, got_ref, reply_ref, back_ref, log_ref,
+                    send1, recv1, send2, recv2):
+    me = lax.axis_index("cp")
+    barrier = pltpu.get_barrier_semaphore()
+
+    def greet(k, carry):
+        pl.semaphore_signal(barrier, inc=1, device_id=(lax.rem(me + k, peers),),
+                            device_id_type=pl.DeviceIdType.MESH)
+        return carry
+
+    lax.fori_loop(1, peers, greet, 0)
+    pl.semaphore_wait(barrier, peers - 1)
+
+    def outward(k):
+        peer = lax.rem(me + k, peers)
+        return pltpu.make_async_remote_copy(
+            src_ref=message_ref.at[peer], dst_ref=got_ref.at[me], send_sem=send1.at[peer], recv_sem=recv1.at[me],
+            device_id=(peer,), device_id_type=pl.DeviceIdType.MESH)
+
+    def inward(k):
+        peer = lax.rem(me + k, peers)
+        return pltpu.make_async_remote_copy(
+            src_ref=message_ref.at[peer], dst_ref=got_ref.at[peer], send_sem=send1.at[peer], recv_sem=recv1.at[peer],
+            device_id=(peer,), device_id_type=pl.DeviceIdType.MESH)
+
+    def reply(k):
+        peer = lax.rem(me + k, peers)
+        return pltpu.make_async_remote_copy(
+            src_ref=reply_ref.at[peer], dst_ref=back_ref.at[me], send_sem=send2.at[peer], recv_sem=recv2.at[me],
+            device_id=(peer,), device_id_type=pl.DeviceIdType.MESH)
+
+    def answer(k):
+        peer = lax.rem(me + k, peers)
+        return pltpu.make_async_remote_copy(
+            src_ref=reply_ref.at[peer], dst_ref=back_ref.at[peer], send_sem=send2.at[peer], recv_sem=recv2.at[peer],
+            device_id=(peer,), device_id_type=pl.DeviceIdType.MESH)
+
+    def each(action):
+        def step(k, carry):
+            action(k)
+            return carry
+        lax.fori_loop(1, peers, step, 0)
+
+    each(lambda k: outward(k).start())
+    got_ref[me] = message_ref[me]
+    each(lambda k: inward(k).wait_recv())
+    log_ref[...] = jnp.zeros_like(log_ref)
     for d in range(peers):
-        out_ref[d] = running.astype(jnp.bfloat16)
-        got = got_ref[d].astype(jnp.float32)
-        log = (got[:, state_dim:state_dim + 1] + got[:, state_dim + 1:state_dim + 2]) + got[:, state_dim + 2:state_dim + 3]
-        running = jnp.exp(log) * running + got
+        logs = got_ref[d, own:own + 3].astype(jnp.float32)
+        log_ref[d:d + 1] = (logs[0:1] + logs[1:2]) + logs[2:3]
+    decays = jnp.exp(log_ref[...]).T
+    running = jnp.zeros((own, got_ref.shape[2]), jnp.float32)
+    for d in range(peers):
+        reply_ref[d] = running.astype(jnp.bfloat16)
+        running = decays[:own, d:d + 1] * running + got_ref[d, :own].astype(jnp.float32)
+    each(lambda k: reply(k).start())
+    back_ref[me] = reply_ref[me]
+    each(lambda k: answer(k).wait_recv())
+    out_ref[...] = back_ref[...]
+    each(lambda k: outward(k).wait_send())
+    each(lambda k: reply(k).wait_send())
 
 
 def output_kernel(head_dim, state_dim, x_ref, part_ref, enter_ref, b_ref, a0_ref, a1_ref, f_ref, d_ref, gain_ref,
                   mix_ref, out_ref, state_ref):
     tokens = x_ref.shape[1]
-    state_ref[...] = enter_ref[:, :state_dim].astype(jnp.float32)
+    state_ref[...] = unpacked(enter_ref[...].astype(jnp.float32), head_dim)
     gain = rows_of(gain_ref[...], head_dim)
 
     def pair(k, carry):
@@ -179,37 +238,53 @@
 
     grid = heads // GROUP
     wide = lambda cols: pl.BlockSpec((group_rows, cols), lambda g: (g, 0))
+    small = pl.BlockSpec((group_rows // 2, 2 * state_dim), lambda g: (g, 0))
     vec = pl.BlockSpec((GROUP, tokens), lambda g: (g, 0))
     vec1 = pl.BlockSpec((GROUP, TILE), lambda g: (g, 0))
     full = lambda array: pl.BlockSpec(array.shape, lambda g: (0,) * array.ndim)
     x, part, message = pl.pallas_call(
         functools.partial(state_kernel, head_dim, state_dim),
         grid=(grid,),
-        in_specs=[wide(tokens), pl.BlockSpec((side.shape[0], group_rows), lambda g: (0, g)), vec, vec, vec1, full(keys)],
-        out_specs=[wide(tokens), wide(tiles * state_dim), wide(2 * state_dim)],
+        in_specs=[wide(tokens), pl.BlockSpec((side.shape[0], group_rows), lambda g: (0, g)), vec, vec, full(keys)],
+        out_specs=[wide(tokens), wide(tiles * state_dim), small],
         out_shape=[
             jax.ShapeDtypeStruct((channels, tokens), bf16),
             jax.ShapeDtypeStruct((channels, tiles * state_dim), bf16),
-            jax.ShapeDtypeStruct((channels, 2 * state_dim), bf16),
+            jax.ShapeDtypeStruct((channels // 2, 2 * state_dim), bf16),
         ],
         scratch_shapes=[pltpu.VMEM((group_rows, TILE), f32), pltpu.VMEM((group_rows, tokens), bf16),
                         pltpu.VMEM((GROUP * 8, tokens), f32)],
         compiler_params=pltpu.CompilerParams(dimension_semantics=("arbitrary",)),
-    )(raw_inputs, side, e, d, total, keys)
-
-    send = message.reshape(peers, channels // peers, 2 * state_dim)
-    got = lax.all_to_all(send, "cp", split_axis=0, concat_axis=0, tiled=True)
-    before = pl.pallas_call(
-        functools.partial(combine_kernel, state_dim),
-        out_shape=jax.ShapeDtypeStruct(got.shape, bf16),
-    )(got)
-    returned = lax.all_to_all(before, "cp", split_axis=0, concat_axis=0, tiled=True)
-    enter = returned.reshape(channels, 2 * state_dim)
+    )(raw_inputs, side, e, d, keys)
+
+    own = channels // 2 // peers
+    logs = jnp.repeat(total[:, 0], head_dim // 2).reshape(peers, own)
+    high = lax.reduce_precision(logs, 8, 7)
+    middle = lax.reduce_precision(logs - high, 8, 7)
+    log_rows = jnp.stack([high, middle, logs - high - middle], axis=1).astype(bf16)
+    filled = -(-(own + 3) // 16) * 16
+    log_rows = jnp.pad(log_rows, ((0, 0), (0, filled - own - 3), (0, 2 * state_dim - own)))
+    send = jnp.concatenate([message.reshape(peers, own, 2 * state_dim), log_rows], axis=1)
+    squares = -(-peers // TILE) * TILE
+    returned = pl.pallas_call(
+        functools.partial(exchange_kernel, peers, own),
+        out_shape=jax.ShapeDtypeStruct((peers, own, 2 * state_dim), bf16),
+        in_specs=[pl.BlockSpec(memory_space=pltpu.VMEM)],
+        out_specs=pl.BlockSpec(memory_space=pltpu.VMEM),
+        scratch_shapes=[
+            pltpu.VMEM((peers, filled, 2 * state_dim), bf16),
+            pltpu.VMEM((peers, own, 2 * state_dim), bf16),
+            pltpu.VMEM((peers, own, 2 * state_dim), bf16),
+            pltpu.VMEM((squares, 2 * state_dim), f32),
+        ] + [pltpu.SemaphoreType.DMA((peers,))] * 4,
+        compiler_params=pltpu.CompilerParams(collective_id=0, has_side_effects=True),
+    )(send)
+    enter = returned.reshape(channels // 2, 2 * state_dim)
     gain = jnp.broadcast_to(skip_gain[:, None], (heads, TILE))
     return pl.pallas_call(
         functools.partial(output_kernel, head_dim, state_dim),
         grid=(grid,),
-        in_specs=[wide(tokens), wide(tiles * state_dim), wide(2 * state_dim), vec, vec, vec, vec, vec, vec1, full(mix)],
+        in_specs=[wide(tokens), wide(tiles * state_dim), small, vec, vec, vec, vec, vec, vec1, full(mix)],
         out_specs=wide(tokens),
         out_shape=jax.ShapeDtypeStruct((channels, tokens), bf16),
         scratch_shapes=[pltpu.VMEM((group_rows, state_dim), f32)],

time: 137 us -> 111 us (0.81)
  the two profiles are of different devices: /device:TPU:0 before, /device:TPU:29 now
where the time goes in v2:
time: 111 us
  Pallas kernels  99.3 us (89%)
  other arithmetic  4.28 us (4%)
  starting transfers between devices  3.68 us (3%)
  local copies, waits for them, and re-layouts  3.58 us (3%)
    pallas_call x1, Pallas kernels, local(): pl.pallas_call(functools.partial(state_kernel, head_dim, state_dim), grid...  41 us
    pallas_call x1, Pallas kernels, local(): pl.pallas_call(functools.partial(exchange_kernel, peers, own), out_shape=...  32 us
    pallas_call x1, Pallas kernels, local(): pl.pallas_call(functools.partial(output_kernel, head_dim, state_dim), gri...  21.7 us
    pallas_call x1, Pallas kernels, local(): pl.pallas_call(functools.partial(prepare_kernel, state_dim), out_shape=[v...  4.55 us
    ppermute x1, starting transfers between devices, local(): halo = lax.ppermute(tail, 'cp', [(s, s + 1) for s in range(peers - 1)])  3.68 us
  transfers between devices with their start and end apart: 1, of which 0 were waited for; matrix products, arithmetic and copies ran while one was open for 2% of the time, Pallas kernels for 4%

profile of v2, /device:TPU:29, one launch (start us, length us, event | category | flops | bytes accessed | tf_op | source)
XLA Modules:
  0.0 110.9 jit_solution(18426733957787653291)
XLA Ops:
  0.0 0.0 copy-start
  0.0 1.5 %slice.6 = bf16[3584,3]{1,0:T(8,128)(2,1)S(1)} slice(bf16[3584,1792]{1,0:T(8,128)(2,1)} %raw_ref.1), slice={[0:3584], [1789:1792]} | slice | bytes 43008 | tf_op jit(solution)/shard_map/slice | solution.py:225
  1.5 0.3 copy.16
  1.9 3.7 %collective-permute-start = (bf16[3,3584]{1,0:T(4,128)(2,1)S(1)}, bf16[3,3584]{1,0:T(4,128)(2,1)S(1)}, u32[]{:S(2)}, u32[]{:S(2)}) collective-permute-start(bf16[3,3584]{1,0:T(4,128)(2,1)S(1)} %bitcast.9), channel_id=1, source_target_pairs={{0,1},{1,2},{2,3},{3,4},{4,5},{5,6},{6,7},{7,8},{8,9},{9,10},{10,1... | collective-permute-start | bytes 64520 | tf_op jit(solution)/shard_map/ppermute | solution.py:226
  5.5 0.7 broadcast_multiply_fusion.1
  6.3 0.8 broadcast_multiply_fusion
  7.1 4.6 %shard_map.73 = (f32[56,1792]{1,0:T(8,128)}, f32[56,1792]{1,0:T(8,128)}, f32[56,1792]{1,0:T(8,128)}, f32[56,1792]{1,0:T(8,128)}, f32[56,1792]{1,0:T(8,128)}, /*i...) custom-call(f32[56,1792]{1,0:T(8,128)} %decay_ref.1, ...), custom_call_target="tpu_custom_call" | custom-call | flops 100000000 | bytes 6000000 | tf_op jit(solution)/shard_map/pallas_call | solution.py:228
  11.7 0.9 slice_reduce_fusion
  12.5 0.1 broadcast_in_dim.4
  12.6 0.1 reshape_reshape.3
  12.7 0.1 fusion.8
  12.9 0.0 collective-permute-done
  12.9 0.7 pad_maximum_fusion.1.side_ref
  13.6 41.0 %shard_map.74 = (bf16[3584,1792]{1,0:T(8,128)(2,1)}, bf16[3584,896]{1,0:T(8,128)(2,1)}, bf16[1792,128]{1,0:T(8,128)(2,1)}) custom-call(bf16[3584,1792]{1,0:T(8,128)(2,1)} %raw_ref.1, f32[8,3584]{1,0:T(8,128)} %pad_maximum_fusion.1.side_ref, f32[56,1792]{1,0:T(8,128)} %get-tuple-element.17.e_ref, f32[56,1792]{1,0:T(8,128)} %get-tuple-element.18.d_ref, ...), custom_call_target="tpu_custom_call" | custom-call | tf_op jit(solution)/shard_map/pallas_call | solution.py:245
  54.6 1.9 %pad_maximum_fusion.message_ref = bf16[32,64,128]{2,1,0:T(8,128)(2,1)} fusion(bf16[32,8,128]{2,1,0:T(8,128)(2,1)S(1)} %fusion.8, bf16[32,56,128]{2,1,0:T(8,128)(2,1)} %bitcast.6), kind=kLoop, calls=%fused_computation | loop fusion | flops 1048576 | bytes 1048576 | tf_op jit(solution)/shard_map/concatenate | solution.py:267
  56.5 32.0 %shard_map.75 = bf16[32,56,128]{2,1,0:T(8,128)(2,1)} custom-call(bf16[32,64,128]{2,1,0:T(8,128)(2,1)} %pad_maximum_fusion.message_ref), custom_call_target="tpu_custom_call" | custom-call | tf_op jit(solution)/shard_map/pallas_call | solution.py:269
  88.5 0.0 copy-done
  88.5 0.7 broadcast_in_dim.5.gain_ref
  89.2 21.7 %shard_map.76 = bf16[3584,1792]{1,0:T(8,128)(2,1)} custom-call(bf16[3584,1792]{1,0:T(8,128)(2,1)} %get-tuple-element.20.x_ref, bf16[3584,896]{1,0:T(8,128)(2,1)} %get-tuple-element.21.part_ref, bf16[1792,128]{1,0:T(8,128)(2,1)} %bitcast.5, f32[56,1792]{1,0:T(8,128)} %get-tuple-element.24.b_ref, f32[56,1792]{1,0:T(8,128)} %get-tuple-element.25.a0_ref, ...), custom_call_target="tpu_custom_call" | custom-call | tf_op jit(solution)/shard_map/pallas_call | solution.py:284
  (5 shorter events, 0.1 us)
Async XLA Ops:
  0.0 88.5 %copy-start = (f32[56]{0:T(128)S(1)}, f32[56]{0:T(128)}, u32[]{:S(2)}) copy-start(f32[56]{0:T(128)} %param.13) | copy-start | bytes 676
  1.9 11.0 %collective-permute-start = (bf16[3,3584]{1,0:T(4,128)(2,1)S(1)}, bf16[3,3584]{1,0:T(4,128)(2,1)S(1)}, u32[]{:S(2)}, u32[]{:S(2)}) collective-permute-start(bf16[3,3584]{1,0:T(4,128)(2,1)S(1)} %bitcast.9), channel_id=1, source_target_pairs={{0,1},{1,2},{2,3},{3,4},{4,5},{5,6},{6,7},{7,8},{8,9},{9,10},{10,1... | collective-permute-start | bytes 64520 | tf_op jit(solution)/shard_map/ppermute | solution.py:226

commit v3 on v2

--- a/solution.py
+++ b/solution.py
@@ -62,28 +62,30 @@
 
 
 def state_kernel(head_dim, state_dim, raw_ref, side_ref, e_ref, d_ref, key_ref, x_ref, part_ref, message_ref,
-                 column_ref, scaled_ref, spread_ref):
+                 column_ref, scaled_ref, spread_ref, weight_ref):
     rows, tokens = raw_ref.shape
     tiles = tokens // TILE
-    side = side_ref[...]
+    halves = jnp.where(lax.broadcasted_iota(jnp.int32, side_ref.shape, 0) < 5, 0.5, 1.0)
+    side = side_ref[...] * halves
     padded = jnp.concatenate([jnp.zeros((TILE - side.shape[0], rows), jnp.float32), side], axis=0)
     column_ref[...] = padded.T
     spread_ref[...] = rows_of(e_ref[...], 8)
+    base = TILE - side.shape[0]
+    for k in range(5):
+        weight_ref[k] = jnp.broadcast_to(column_ref[:, base + k:base + k + 1], (rows, TILE))
     step_rows = head_dim // 2
-    base = TILE - side.shape[0]
 
     def convolve(group, carry):
         start = pl.multiple_of(group * step_rows, step_rows)
         head = group // 2
         lane = lax.broadcasted_iota(jnp.int32, (step_rows, TILE), 1)
         columns = column_ref[pl.ds(start, step_rows), :]
-        w0, w1, w2, w3, bias = [
-            jnp.broadcast_to(columns[:, base + k:base + k + 1], (step_rows, TILE)) for k in range(5)
-        ]
+        w0, w1, w2, w3, bias = [weight_ref[k, pl.ds(start, step_rows), :] for k in range(5)]
         before1 = pltpu.roll(columns, 1, 1)
         before2 = pltpu.roll(w1 * columns + w0 * before1, 2, 1)
         for t in range(tiles):
             span = slice(t * TILE, (t + 1) * TILE)
+            w0, w1, w2, w3, bias = [weight_ref[k, pl.ds(start, step_rows), :] for k in range(5)]
             now = raw_ref[pl.ds(start, step_rows), span].astype(jnp.float32)
             turned = pltpu.roll(now, 1, 1)
             late1 = jnp.where(lane < 1, before1, turned)
@@ -99,13 +101,17 @@
         return carry
 
     lax.fori_loop(0, rows // step_rows, convolve, 0)
-    state = jnp.zeros((rows, state_dim), jnp.float32)
+    low = lax.broadcasted_iota(jnp.int32, (d_ref.shape[0], TILE), 1) < state_dim
+    both = jnp.zeros((rows, TILE), jnp.float32)
+    last = d_ref[:, :TILE]
     for k in range(tokens // PAIR):
         part = jnp.dot(scaled_ref[:, k * PAIR:(k + 1) * PAIR], key_ref[k], preferred_element_type=jnp.float32)
         part_ref[:, k * TILE:(k + 1) * TILE] = part.astype(jnp.bfloat16)
-        for i in range(2):
-            decay = rows_of(d_ref[:, (2 * k + i) * TILE:(2 * k + i) * TILE + state_dim], head_dim)
-            state = decay * state + part[:, i * state_dim:(i + 1) * state_dim]
+        even = d_ref[:, 2 * k * TILE:(2 * k + 1) * TILE]
+        odd = d_ref[:, (2 * k + 1) * TILE:(2 * k + 2) * TILE]
+        both = part if k == 0 else rows_of(even * jnp.where(low, last, odd), head_dim) * both + part
+        last = odd
+    state = both[:, :state_dim] * rows_of(last, head_dim)[:, :state_dim] + both[:, state_dim:]
     message_ref[...] = packed(state, head_dim).astype(jnp.bfloat16)
 
 
@@ -122,10 +128,12 @@
         2 * rows, width // 2)
 
 
-def exchange_kernel(peers, own, message_ref, out_ref, got_ref, reply_ref, back_ref, log_ref,
+def exchange_kernel(peers, own, state_ref, extra_ref, out_ref, message_ref, got_ref, reply_ref, back_ref, log_ref,
                     send1, recv1, send2, recv2):
     me = lax.axis_index("cp")
     barrier = pltpu.get_barrier_semaphore()
+    message_ref[:, :own] = state_ref[...]
+    message_ref[:, own:] = extra_ref[...]
 
     def greet(k, carry):
         pl.semaphore_signal(barrier, inc=1, device_id=(lax.rem(me + k, peers),),
@@ -234,7 +242,7 @@
         ],
         cost_estimate=pl.CostEstimate(flops=100000000, bytes_accessed=6000000, transcendentals=0),
     )(log_decay, step_size, state_maps)
-    side = jnp.concatenate([0.5 * conv_weight, 0.5 * conv_bias[None], halo.astype(f32)], axis=0)
+    side = jnp.concatenate([conv_weight, conv_bias[None], halo.astype(f32)], axis=0)
 
     grid = heads // GROUP
     wide = lambda cols: pl.BlockSpec((group_rows, cols), lambda g: (g, 0))
@@ -253,7 +261,8 @@
             jax.ShapeDtypeStruct((channels // 2, 2 * state_dim), bf16),
         ],
         scratch_shapes=[pltpu.VMEM((group_rows, TILE), f32), pltpu.VMEM((group_rows, tokens), bf16),
-                        pltpu.VMEM((GROUP * 8, tokens), f32)],
+                        pltpu.VMEM((GROUP * 8, tokens), f32),
+                        pltpu.VMEM((5, group_rows, TILE), f32)],
         compiler_params=pltpu.CompilerParams(dimension_semantics=("arbitrary",)),
     )(raw_inputs, side, e, d, keys)
 
@@ -264,21 +273,21 @@
     log_rows = jnp.stack([high, middle, logs - high - middle], axis=1).astype(bf16)
     filled = -(-(own + 3) // 16) * 16
     log_rows = jnp.pad(log_rows, ((0, 0), (0, filled - own - 3), (0, 2 * state_dim - own)))
-    send = jnp.concatenate([message.reshape(peers, own, 2 * state_dim), log_rows], axis=1)
     squares = -(-peers // TILE) * TILE
     returned = pl.pallas_call(
         functools.partial(exchange_kernel, peers, own),
         out_shape=jax.ShapeDtypeStruct((peers, own, 2 * state_dim), bf16),
-        in_specs=[pl.BlockSpec(memory_space=pltpu.VMEM)],
+        in_specs=[pl.BlockSpec(memory_space=pltpu.VMEM)] * 2,
         out_specs=pl.BlockSpec(memory_space=pltpu.VMEM),
         scratch_shapes=[
+            pltpu.VMEM((peers, filled, 2 * state_dim), bf16),
             pltpu.VMEM((peers, filled, 2 * state_dim), bf16),
             pltpu.VMEM((peers, own, 2 * state_dim), bf16),
             pltpu.VMEM((peers, own, 2 * state_dim), bf16),
             pltpu.VMEM((squares, 2 * state_dim), f32),
         ] + [pltpu.SemaphoreType.DMA((peers,))] * 4,
         compiler_params=pltpu.CompilerParams(collective_id=0, has_side_effects=True),
-    )(send)
+    )(message.reshape(peers, own, 2 * state_dim), log_rows)
     enter = returned.reshape(channels // 2, 2 * state_dim)
     gain = jnp.broadcast_to(skip_gain[:, None], (heads, TILE))
     return pl.pallas_call(

time: 111 us -> 106 us (0.955)
  Pallas kernels: 99.3 us -> 95.7 us
  other arithmetic: 4.28 us -> 2.28 us
    pallas_call x1, Pallas kernels: 41 us -> 37.1 us  [local(): pl.pallas_call(functools.partial(state_kernel, head_dim, state_dim), grid...]
    mul x2 -> x0, other arithmetic: 1.55 us -> none  [the longest x1 0.83 us: local(): 0.5 * conv_weight]
    concatenate x2 -> x1, other arithmetic: 2.57 us -> 1.51 us  [local(): jnp.concatenate([conv_weight, conv_bias[None], halo.astype(f32)], axis=0)]
where the time goes in v3:
time: 106 us
  Pallas kernels  95.7 us (90%)
  local copies, waits for them, and re-layouts  4.28 us (4%)
  starting transfers between devices  3.68 us (3%)
  other arithmetic  2.28 us (2%)
    pallas_call x1, Pallas kernels, local(): pl.pallas_call(functools.partial(state_kernel, head_dim, state_dim), grid...  37.1 us
    pallas_call x1, Pallas kernels, local(): pl.pallas_call(functools.partial(exchange_kernel, peers, own), out_shape=...  32.3 us
    pallas_call x1, Pallas kernels, local(): pl.pallas_call(functools.partial(output_kernel, head_dim, state_dim), gri...  21.7 us
    pallas_call x1, Pallas kernels, local(): pl.pallas_call(functools.partial(prepare_kernel, state_dim), out_shape=[v...  4.55 us
    ppermute x1, starting transfers between devices, local(): halo = lax.ppermute(tail, 'cp', [(s, s + 1) for s in range(peers - 1)])  3.68 us
  transfers between devices with their start and end apart: 1, of which 0 were waited for; matrix products, arithmetic and copies ran while one was open for 2% of the time, Pallas kernels for 4%

profile of v3, /device:TPU:29, one launch (start us, length us, event | category | flops | bytes accessed | tf_op | source)
XLA Modules:
  0.0 106.0 jit_solution(17706350124812780594)
XLA Ops:
  0.0 0.0 copy-start
  0.0 1.5 %slice.6 = bf16[3584,3]{1,0:T(8,128)(2,1)S(1)} slice(bf16[3584,1792]{1,0:T(8,128)(2,1)} %raw_ref.1), slice={[0:3584], [1789:1792]} | slice | bytes 43008 | tf_op jit(solution)/shard_map/slice | solution.py:233
  1.5 0.3 copy.16
  1.9 3.7 %collective-permute-start = (bf16[3,3584]{1,0:T(4,128)(2,1)S(1)}, bf16[3,3584]{1,0:T(4,128)(2,1)S(1)}, u32[]{:S(2)}, u32[]{:S(2)}) collective-permute-start(bf16[3,3584]{1,0:T(4,128)(2,1)S(1)} %bitcast.9), channel_id=1, source_target_pairs={{0,1},{1,2},{2,3},{3,4},{4,5},{5,6},{6,7},{7,8},{8,9},{9,10},{10,1... | collective-permute-start | bytes 64520 | tf_op jit(solution)/shard_map/ppermute | solution.py:234
  5.5 4.6 %shard_map.73 = (f32[56,1792]{1,0:T(8,128)}, f32[56,1792]{1,0:T(8,128)}, f32[56,1792]{1,0:T(8,128)}, f32[56,1792]{1,0:T(8,128)}, f32[56,1792]{1,0:T(8,128)}, /*i...) custom-call(f32[56,1792]{1,0:T(8,128)} %decay_ref.1, ...), custom_call_target="tpu_custom_call" | custom-call | flops 100000000 | bytes 6000000 | tf_op jit(solution)/shard_map/pallas_call | solution.py:236
  10.1 0.9 slice_reduce_fusion
  11.0 0.1 broadcast_in_dim.13
  11.0 0.1 reshape_reshape.3
  11.2 0.7 fusion.8.extra_ref
  11.9 0.7 broadcast_in_dim.12
  12.6 0.0 collective-permute-done
  12.7 1.5 %pad_maximum_fusion.side_ref = f32[8,3584]{1,0:T(8,128)} fusion(f32[3,3584]{1,0:T(4,128)S(1)} %convert_element_type.6, f32[1,3584]{1,0:T(1,128)S(1)} %broadcast_in_dim.12, f32[4,3584]{1,0:T(4,128)} %param.11), kind=kLoop, calls=%fused_computation.6 | loop fusion | flops 57344 | bytes 229376 | tf_op jit(solution)/shard_map/concatenate | solution.py:245
  14.2 37.1 %shard_map.74 = (bf16[3584,1792]{1,0:T(8,128)(2,1)}, bf16[3584,896]{1,0:T(8,128)(2,1)}, bf16[1792,128]{1,0:T(8,128)(2,1)}) custom-call(bf16[3584,1792]{1,0:T(8,128)(2,1)} %raw_ref.1, f32[8,3584]{1,0:T(8,128)} %pad_maximum_fusion.side_ref, f32[56,1792]{1,0:T(8,128)} %get-tuple-element.17.e_ref, f32[56,1792]{1,0:T(8,128)} %get-tuple-element.18.d_ref, ...), custom_call_target="tpu_custom_call" | custom-call | tf_op jit(solution)/shard_map/pallas_call | solution.py:253
  51.3 32.3 %shard_map.75 = bf16[32,56,128]{2,1,0:T(8,128)(2,1)} custom-call(bf16[32,56,128]{2,1,0:T(8,128)(2,1)} %bitcast.6, bf16[32,8,128]{2,1,0:T(8,128)(2,1)} %fusion.8.extra_ref), custom_call_target="tpu_custom_call" | custom-call | tf_op jit(solution)/shard_map/pallas_call | solution.py:277
  83.6 0.0 copy-done
  83.6 0.7 broadcast_in_dim.14.gain_ref
  84.3 21.7 %shard_map.76 = bf16[3584,1792]{1,0:T(8,128)(2,1)} custom-call(bf16[3584,1792]{1,0:T(8,128)(2,1)} %get-tuple-element.20.x_ref, bf16[3584,896]{1,0:T(8,128)(2,1)} %get-tuple-element.21.part_ref, bf16[1792,128]{1,0:T(8,128)(2,1)} %bitcast.5, f32[56,1792]{1,0:T(8,128)} %get-tuple-element.24.b_ref, f32[56,1792]{1,0:T(8,128)} %get-tuple-element.25.a0_ref, ...), custom_call_target="tpu_custom_call" | custom-call | tf_op jit(solution)/shard_map/pallas_call | solution.py:293
  (4 shorter events, 0.1 us)
Async XLA Ops:
  0.0 83.6 %copy-start = (f32[56]{0:T(128)S(1)}, f32[56]{0:T(128)}, u32[]{:S(2)}) copy-start(f32[56]{0:T(128)} %param.13) | copy-start | bytes 676
  1.9 10.8 %collective-permute-start = (bf16[3,3584]{1,0:T(4,128)(2,1)S(1)}, bf16[3,3584]{1,0:T(4,128)(2,1)S(1)}, u32[]{:S(2)}, u32[]{:S(2)}) collective-permute-start(bf16[3,3584]{1,0:T(4,128)(2,1)S(1)} %bitcast.9), channel_id=1, source_target_pairs={{0,1},{1,2},{2,3},{3,4},{4,5},{5,6},{6,7},{7,8},{8,9},{9,10},{10,1... | collective-permute-start | bytes 64520 | tf_op jit(solution)/shard_map/ppermute | solution.py:234
